TPU v7x, 512 devices: a whole 4x8x8 slice. The times are simulated.
512 devices in a mesh: gx: 4 (over x), gy: 8 (over z), gz: 16 (over y, core).
Axes of the slice: x: 4, y: 8, z: 8, core: 2. Of those that a mesh axis runs over, the one named last changes fastest.
Arguments:
- positions: float32 [3, 262144], P(None, ('gx', 'gy', 'gz')), may hold values from -6 to 6
- frames: float32 [128, 3, 4096], P(None, None, ('gy', 'gz')), may hold values from -6 to 6
- path_slot: int32 [512, 32], P(('gx', 'gy', 'gz')), may hold values from 0 to 511, as said below
- path_count: int32 [512], replicated, may hold values from 1 to 32, 4096 in all
- path_order: int32 [4096], replicated, may hold values from 0 to 4095, each once
- frame_rank: int32 [128], replicated, may hold values from 0 to 127, each once
Outputs:
- forces: float32 [3, 262144], P(None, ('gx', 'gy', 'gz'))
- path_cv: float32 [2], replicated
Inputs may be any that keep to these rules, and one draw needn't show every extreme that they name: `path_slot`: within one domain's row the 32 local atom indices are all different.
All inputs are finite; a program needn't handle non-finite values.
Results may differ from a plain program's by a relative error of at most 0.00013.
Values sent between devices are 32-bit elements; how exact they have to be, the bound alone decides.
No kernel may reach another device: no remote copies, remote signals or barrier semaphores. Data moves between devices by JAX's collectives and lax.ppermute only.
A program may use at most 64 MiB of HBM per device.

v0:
```python
import jax
import jax.numpy as jnp
from jax import lax
from jax.sharding import Mesh
from jax.sharding import PartitionSpec as P

P_SIZE = 4096
GX_GY_GZ = ("gx", "gy", "gz_0", "gz_1")
GY_GZ = ("gy", "gz_0", "gz_1")
STRENGTH = 20.0
S_HOME = 0.5
KAPPA_S = 0.5
KAPPA_Z = 0.05
PAIR_SCALE = 0.02
WIDTH_SQ = 4.0


def one_axis_at_a_time(array, axes):
    for axis in axes:
        array = lax.psum(array, axis)
    return array


def pair_block(block_pos, all_pos):
    diff = block_pos[:, :, None] - all_pos[:, None, :]
    dist_sq = jnp.sum(diff * diff, axis=0)
    weight = PAIR_SCALE * jnp.exp(-dist_sq / WIDTH_SQ)
    return jnp.sum(weight[None] * diff, axis=2)


def domain_forces(local):
    atoms = local.shape[1]
    rows = 256
    blocks = local.reshape(3, atoms // rows, rows).transpose(1, 0, 2)
    result = lax.map(lambda block: pair_block(block, local), blocks)
    return result.transpose(1, 0, 2).reshape(3, atoms)


def slot_ids(path_count, path_order, slots):
    offsets = jnp.cumsum(path_count) - path_count
    steps_k = jnp.arange(slots, dtype=jnp.int32)
    live = steps_k[None, :] < path_count[:, None]
    place = jnp.clip(offsets[:, None] + steps_k[None, :], 0, P_SIZE - 1)
    ids = jnp.where(live, path_order[place], -1)
    return (ids, live)


def cv_terms(dist, frame_rank):
    frames_n = dist.shape[0]
    expo = -STRENGTH * dist
    top = jnp.max(expo)
    expd = jnp.exp(expo - top)
    total = jnp.sum(expd)
    weight = expd / total
    progress_rank = frame_rank.astype(jnp.float32) / (frames_n - 1.0)
    s_value = jnp.sum(progress_rank * weight)
    z_value = -(top + jnp.log(total)) / STRENGTH
    grads = (
        KAPPA_S * P_SIZE * (s_value - S_HOME) * -STRENGTH * weight * (progress_rank - s_value)
        + KAPPA_Z * P_SIZE * z_value * weight
    )
    return (s_value, z_value, grads)


def summed_terms(partial_value, frame_rank):
    dist = one_axis_at_a_time(partial_value, GX_GY_GZ)
    return cv_terms(dist, frame_rank)


def body(positions, frames, path_slot, path_count, path_order, frame_rank):
    slots = path_slot.shape[1]
    local_slot = path_slot[0]
    ids, live = slot_ids(path_count, path_order, slots)
    path_pos = jnp.take(positions, local_slot, axis=1)
    here = lax.axis_index(GX_GY_GZ)
    my_ids = lax.dynamic_slice_in_dim(ids, here, 1, 0)[0]
    mask = lax.dynamic_slice_in_dim(live, here, 1, 0)[0].astype(jnp.float32)
    whole = lax.all_gather(frames, GY_GZ, axis=2, tiled=True)
    refs = jnp.take(whole, jnp.clip(my_ids, 0, P_SIZE - 1), axis=2)
    delta = path_pos[None] - refs
    partial_value = jnp.sum(jnp.sum(delta * delta, axis=1) * mask[None], axis=1) / P_SIZE
    s_value, z_value, grads = summed_terms(partial_value, frame_rank)
    bias = (
        -(2.0 / P_SIZE)
        * jnp.einsum("f,fcm->cm", grads, delta, precision=lax.Precision.HIGHEST)
        * mask[None]
    )
    forces = domain_forces(positions)
    forces = forces.at[:, local_slot].add(bias)
    return (forces, jnp.stack([s_value, z_value]))


def solution(mesh):
    finer = Mesh(
        mesh.devices.reshape(mesh.shape["gx"], mesh.shape["gy"], 8, 2), ("gx", "gy", "gz_0", "gz_1")
    )
    return jax.shard_map(
        body,
        mesh=finer,
        in_specs=(P(None, GX_GY_GZ), P(None, None, GY_GZ), P(GX_GY_GZ, None), P(), P(), P()),
        out_specs=(P(None, GX_GY_GZ), P()),
        check_vma=False,
    )
```

profile of v0, /device:TPU:1, one launch (start us, length us, event | category | flops | bytes accessed | tf_op | source)
XLA Modules:
  0.0 190.1 jit_solution(15374449258505947878)
XLA Ops:
  7.2 0.0 copy-start
  7.2 0.0 all-gather.2.cloned.1.call-start
  7.2 0.7 all-gather.2.cloned.1.call-update
  7.9 1.0 reduce-window.9
  8.9 0.1 slice.7
  9.0 0.1 slice_reduce_fusion
  9.1 0.8 bitcast_subtract_fusion.1
  9.9 0.1 compare_select_fusion
  10.0 0.1 reshape.176
  10.2 0.0 copy-done
  10.2 0.0 copy-start.1
  10.2 90.5 %gather_fusion.1 = s32[16384]{0:T(1024)S(1)} fusion(s32[4096]{0:T(1024)S(1)} %copy-done, s32[16384]{0:T(1024)S(1)} %broadcast_clamp_fusion), kind=kCustom, calls=%fused_computation.1 | custom fusion | bytes 196608 | tf_op jit(solution)/shard_map/gather | solution.py:44
  100.8 0.1 reshape.175
  100.9 0.0 copy-done.1
  100.9 0.1 copy.21
  101.0 0.0 copy-start.4
  101.0 0.0 copy-start.2
  101.1 1.5 while.10
  101.1 0.2 fusion.25
  101.3 0.1 exponential_multiply_fusion.2
  101.4 0.4 fusion.26
  101.8 0.2 fusion.25
  102.0 0.1 exponential_multiply_fusion.2
  102.1 0.4 fusion.26
  102.5 0.1 copy.20
  102.7 0.0 copy-done.4
  102.7 0.6 gather_fusion
  103.3 0.0 copy-done.2
  103.3 0.1 iota_compare_fusion
  103.5 0.1 select_bitcast_fusion
  103.6 0.0 copy-start.3
  103.6 0.0 all-gather.2.cloned.1.call-done
  103.6 10.7 %copy.22 = f32[128,3,4096]{0,1,2:T(4,128)} copy(f32[128,3,4096]{0,2,1:T(8,128)} %all-gather.2.cloned.1.call-done) | data formatting | bytes 12582912 | tf_op jit(solution)/shard_map/all_gather | solution.py:78
  114.3 4.0 %gather_fusion.2 = f32[32,128,3]{1,2,0:T(4,128)S(1)} fusion(f32[128,3,4096]{0,1,2:T(4,128)} %copy.22, s32[1024]{0:T(1024)S(1)} %pad_clamp_fusion), kind=kCustom, calls=%fused_computation.2 | custom fusion | bytes 98432 | tf_op jit(solution)/shard_map/jit(_take)/gather | solution.py:79
  118.3 0.1 multiply_reduce_fusion
  118.4 0.1 multiply_reduce_fusion.1
  118.5 9.3 %psum.28 = f32[128]{0:T(128)S(1)} all-reduce(f32[128]{0:T(128)S(1)} %broadcast_multiply_fusion), channel_id=1, replica_groups=mesh['gx'=4,'gy'=8,'gz_0'=8,'gz_1'=2] {'gx'}, use_global_device_ids=true, to_apply=%region_8.9 | all-reduce | flops 128 | bytes 1024 | tf_op jit(solution)/shard_map/psum | solution.py:20
  127.8 19.5 %psum.29 = f32[128]{0:T(128)S(1)} all-reduce(f32[128]{0:T(128)S(1)} %psum.28), channel_id=1, replica_groups=mesh['gx'=4,'gy'=8,'gz_0'=8,'gz_1'=2] {'gy'}, use_global_device_ids=true, to_apply=%region_9.10 | all-reduce | flops 128 | bytes 1024 | tf_op jit(solution)/shard_map/psum | solution.py:20
  147.3 13.8 %psum.30 = f32[128]{0:T(128)S(1)} all-reduce(f32[128]{0:T(128)S(1)} %psum.29), channel_id=1, replica_groups=mesh['gx'=4,'gy'=8,'gz_0'=8,'gz_1'=2] {'gz_0'}, use_global_device_ids=true, to_apply=%region_10.11 | all-reduce | flops 128 | bytes 1024 | tf_op jit(solution)/shard_map/psum | solution.py:20
  161.1 12.3 %psum.31 = f32[128]{0:T(128)S(1)} all-reduce(f32[128]{0:T(128)S(1)} %psum.30), channel_id=1, replica_groups=mesh['gx'=4,'gy'=8,'gz_0'=8,'gz_1'=2] {'gz_1'}, use_global_device_ids=true, to_apply=%region_11.12 | all-reduce | flops 128 | bytes 1024 | tf_op jit(solution)/shard_map/psum | solution.py:20
  173.4 0.6 multiply_reduce_fusion.3
  174.0 1.3 fusion.21
  176.6 0.0 copy-done.3
  176.6 2.0 %multiply_reduce_fusion.2 = (f32[]{:T(128)}, f32[128]{0:T(128)S(1)}) fusion(s32[128]{0:T(128)S(1)} %copy-done.3, f32[]{:T(128)} %fusion.21, f32[]{:T(128)} %multiply_reduce_fusion.3, f32[128]{0:T(128)S(1)} %psum.31), kind=kLoop, calls=%fused_computation.47 | loop fusion | flops 895 | bytes 1548 | tf_op jit(solution)/shard_map/reduce_sum | solution.py:56
  179.3 0.9 fusion.2
  180.2 0.1 copy.25
  180.3 1.0 scatter_custom_fusion
  181.3 0.7 copy.23
  182.0 1.3 pad_maximum_fusion
  (15 shorter events, 0.2 us)
Async XLA Ops:
  7.2 3.0 %copy-start = (s32[4096]{0:T(1024)S(1)}, s32[4096]{0:T(1024)}, u32[]{:S(2)}) copy-start(s32[4096]{0:T(1024)} %param.12) | copy-start | bytes 49156
  7.2 96.4 %all-gather.2.cloned.1.call-start = ((), (), s32[]{:S(2)}) async-start(), calls=%async_computation | async-start | bytes 6340608 | tf_op jit(solution)/shard_map/all_gather | solution.py:78
  10.2 90.7 %copy-start.1 = (f32[3,512]{1,0:T(4,128)S(1)}, f32[3,512]{1,0:T(4,128)}, u32[]{:S(2)}) copy-start(f32[3,512]{1,0:T(4,128)} %param.8) | copy-start | bytes 18436
  101.0 1.6 copy-start.4
  101.0 2.2 %copy-start.2 = (s32[512]{0:T(512)S(1)}, s32[512]{0:T(512)}, u32[]{:S(2)}) copy-start(s32[512]{0:T(512)} %param.11) | copy-start | bytes 6148
  103.6 73.0 %copy-start.3 = (s32[128]{0:T(128)S(1)}, s32[128]{0:T(128)}, u32[]{:S(2)}) copy-start(s32[128]{0:T(128)} %param.13) | copy-start | bytes 1540
Sparse Core Ops, SparseCore 0:
  11.2 91.8 all-gather.1
where the time goes:
time: 191 us; the launch traced here: 190 us
  local copies, waits for them, and re-layouts  107 us (56%)
  blocking collectives  54.9 us (29%)
  between operations  16.3 us (9%)
  other arithmetic  9.86 us (5%)
    gather x2, local copies, waits for them, and re-layouts, slot_ids(): ids = jnp.where(live, path_order[place], -1)  90.7 us
    psum x4, blocking collectives, one_axis_at_a_time(): array = lax.psum(array, axis)  54.9 us
    all_gather x1, local copies, waits for them, and re-layouts, body(): whole = lax.all_gather(frames, GY_GZ, axis=2, tiled=True)  10.7 us
    gather x1, local copies, waits for them, and re-layouts, body(): refs = jnp.take(whole, jnp.clip(my_ids, 0, P_SIZE - 1), axis=2)  3.99 us
  transfers between devices with their start and end apart: 1, of which 0 were waited for; matrix products, arithmetic and copies ran while one was open for 50% of the time, Pallas kernels for 0%

commit v1 on v0

--- a/solution.py
+++ b/solution.py
@@ -75,7 +75,8 @@
     here = lax.axis_index(GX_GY_GZ)
     my_ids = lax.dynamic_slice_in_dim(ids, here, 1, 0)[0]
     mask = lax.dynamic_slice_in_dim(live, here, 1, 0)[0].astype(jnp.float32)
-    whole = lax.all_gather(frames, GY_GZ, axis=2, tiled=True)
+    parts = lax.all_gather(frames, GY_GZ)
+    whole = jnp.concatenate(parts, axis=2)
     refs = jnp.take(whole, jnp.clip(my_ids, 0, P_SIZE - 1), axis=2)
     delta = path_pos[None] - refs
     partial_value = jnp.sum(jnp.sum(delta * delta, axis=1) * mask[None], axis=1) / P_SIZE

time: 191 us -> 206 us (1.079)
  local copies, waits for them, and re-layouts: 107 us -> 123 us
  blocking collectives: 54.9 us -> 52.8 us
  waiting for transfers between devices: 0.68 us -> 2.77 us
    reshape x0 -> x2, local copies, waits for them, and re-layouts: none -> 22.3 us  [body(): whole = jnp.concatenate(parts, axis=2)]
    all_gather x1 -> x0, local copies, waits for them, and re-layouts: 10.7 us -> none  [body(): whole = lax.all_gather(frames, GY_GZ, axis=2, tiled=True)]
    unnamed x12 -> x13, local copies, waits for them, and re-layouts: 0.89 us -> 4.76 us
    all_gather x1, waiting for transfers between devices: 0.01 us -> 2.09 us  [body(): parts = lax.all_gather(frames, GY_GZ)]
    psum x4, blocking collectives: 54.9 us -> 52.8 us  [one_axis_at_a_time(): array = lax.psum(array, axis)]
  transfers between devices with their start and end apart: 1 -> 1, of which waited for: 0 -> 1; matrix products, arithmetic and copies ran while one was open for 50% -> 46% of each run, Pallas kernels for 0% -> 0%
where the time goes in v1:
time: 206 us
  local copies, waits for them, and re-layouts  123 us (60%)
  blocking collectives  52.8 us (26%)
  between operations  16.3 us (8%)
  other arithmetic  9.86 us (5%)
  waiting for transfers between devices  2.77 us (1%)
    gather x2, local copies, waits for them, and re-layouts, slot_ids(): ids = jnp.where(live, path_order[place], -1)  90.7 us
    psum x4, blocking collectives, one_axis_at_a_time(): array = lax.psum(array, axis)  52.8 us
    reshape x2, local copies, waits for them, and re-layouts, body(): whole = jnp.concatenate(parts, axis=2)  22.3 us
    unnamed x13, local copies, waits for them, and re-layouts  4.76 us
  transfers between devices with their start and end apart: 1, of which 1 were waited for; matrix products, arithmetic and copies ran while one was open for 46% of the time, Pallas kernels for 0%

profile of v1, /device:TPU:1, one launch (start us, length us, event | category | flops | bytes accessed | tf_op | source)
XLA Modules:
  0.0 205.6 jit_solution(1242888163513133791)
XLA Ops:
  7.2 0.0 copy-start
  7.2 0.0 all-gather.3.cloned.1.call-start
  7.2 0.7 all-gather.3.cloned.1.call-update
  7.9 1.0 reduce-window.9
  8.9 0.1 slice.7
  9.0 0.1 slice_reduce_fusion
  9.1 0.8 bitcast_subtract_fusion.1
  9.9 0.1 compare_select_fusion
  10.0 0.1 reshape.184
  10.2 0.0 copy-done
  10.2 0.0 copy-start.1
  10.2 90.5 %gather_fusion.1 = s32[16384]{0:T(1024)S(1)} fusion(s32[4096]{0:T(1024)S(1)} %copy-done, s32[16384]{0:T(1024)S(1)} %broadcast_clamp_fusion), kind=kCustom, calls=%fused_computation.1 | custom fusion | bytes 196608 | tf_op jit(solution)/shard_map/gather | solution.py:44
  100.8 0.1 reshape.183
  100.9 0.0 copy-done.1
  100.9 0.1 copy.27
  101.0 0.0 copy-start.4
  101.0 0.0 copy-start.2
  101.1 1.4 while.10
  101.1 0.2 fusion.25
  101.3 0.1 exponential_multiply_fusion.2
  101.4 0.4 fusion.26
  101.8 0.2 fusion.25
  102.0 0.1 exponential_multiply_fusion.2
  102.1 0.4 fusion.26
  102.5 0.1 copy.26
  102.7 0.0 copy-done.4
  102.7 0.6 gather_fusion
  103.3 0.0 copy-done.2
  103.3 0.1 iota_compare_fusion
  103.5 0.1 select_bitcast_fusion
  103.6 2.1 %all-gather.3.cloned.1.call-done = f32[16384,3,32]{0,2,1:T(8,128)} async-done(((f32[128,3,32]{0,2,1:T(8,128)}), f32[16384,3,32]{0,2,1:T(8,128)}) %all-gather.3.cloned.1.call-update) | async-done | bytes 6291472 | tf_op jit(solution)/shard_map/all_gather | solution.py:78
  105.7 3.9 %copy.33 = f32[12,8,128,128]{3,2,1,0:T(8,128)S(1)} copy(f32[12,8,128,128]{3,1,2,0:T(8,128)} %bitcast.63) | data formatting | bytes 12582912
  109.6 3.6 %copy.28 = f32[128,3,128,32]{0,3,2,1:T(8,128)S(1)} copy(f32[128,3,128,32]{0,2,3,1:T(8,128)S(1)} %bitcast.61) | data formatting | bytes 12582912 | tf_op jit(solution)/shard_map/reshape | solution.py:79
  113.2 0.0 copy-start.3
  113.2 18.7 %copy.29 = f32[128,3,4096]{0,1,2:T(4,128)} copy(f32[128,3,4096]{0,2,1:T(8,128)S(1)} %bitcast.62) | data formatting | bytes 12582912 | tf_op jit(solution)/shard_map/reshape | solution.py:79
  131.9 4.0 %gather_fusion.2 = f32[32,128,3]{1,2,0:T(4,128)S(1)} fusion(f32[128,3,4096]{0,1,2:T(4,128)} %copy.29, s32[1024]{0:T(1024)S(1)} %pad_clamp_fusion), kind=kCustom, calls=%fused_computation.2 | custom fusion | bytes 98432 | tf_op jit(solution)/shard_map/jit(_take)/gather | solution.py:80
  135.9 0.1 multiply_reduce_fusion
  136.0 0.1 multiply_reduce_fusion.1
  136.1 8.3 %psum.28 = f32[128]{0:T(128)S(1)} all-reduce(f32[128]{0:T(128)S(1)} %broadcast_multiply_fusion), channel_id=1, replica_groups=mesh['gx'=4,'gy'=8,'gz_0'=8,'gz_1'=2] {'gx'}, use_global_device_ids=true, to_apply=%region_8.9 | all-reduce | flops 128 | bytes 1024 | tf_op jit(solution)/shard_map/psum | solution.py:20
  144.4 18.4 %psum.29 = f32[128]{0:T(128)S(1)} all-reduce(f32[128]{0:T(128)S(1)} %psum.28), channel_id=1, replica_groups=mesh['gx'=4,'gy'=8,'gz_0'=8,'gz_1'=2] {'gy'}, use_global_device_ids=true, to_apply=%region_9.10 | all-reduce | flops 128 | bytes 1024 | tf_op jit(solution)/shard_map/psum | solution.py:20
  162.8 13.8 %psum.30 = f32[128]{0:T(128)S(1)} all-reduce(f32[128]{0:T(128)S(1)} %psum.29), channel_id=1, replica_groups=mesh['gx'=4,'gy'=8,'gz_0'=8,'gz_1'=2] {'gz_0'}, use_global_device_ids=true, to_apply=%region_10.11 | all-reduce | flops 128 | bytes 1024 | tf_op jit(solution)/shard_map/psum | solution.py:20
  176.6 12.3 %psum.31 = f32[128]{0:T(128)S(1)} all-reduce(f32[128]{0:T(128)S(1)} %psum.30), channel_id=1, replica_groups=mesh['gx'=4,'gy'=8,'gz_0'=8,'gz_1'=2] {'gz_1'}, use_global_device_ids=true, to_apply=%region_11.12 | all-reduce | flops 128 | bytes 1024 | tf_op jit(solution)/shard_map/psum | solution.py:20
  188.9 0.6 multiply_reduce_fusion.3
  189.5 1.3 fusion.21
  192.1 0.0 copy-done.3
  192.1 2.0 multiply_reduce_fusion.2
  194.8 0.9 fusion.2
  195.7 0.1 copy.32
  195.8 1.0 scatter_custom_fusion
  196.8 0.7 copy.30
  197.5 1.3 pad_maximum_fusion
  (15 shorter events, 0.2 us)
Async XLA Ops:
  7.2 3.0 %copy-start = (s32[4096]{0:T(1024)S(1)}, s32[4096]{0:T(1024)}, u32[]{:S(2)}) copy-start(s32[4096]{0:T(1024)} %param.12) | copy-start | bytes 49156
  7.2 98.5 %all-gather.3.cloned.1.call-start = ((), (), s32[]{:S(2)}) async-start(), calls=%async_computation | async-start | bytes 6340608 | tf_op jit(solution)/shard_map/all_gather | solution.py:78
  10.2 90.7 %copy-start.1 = (f32[3,512]{1,0:T(4,128)S(1)}, f32[3,512]{1,0:T(4,128)}, u32[]{:S(2)}) copy-start(f32[3,512]{1,0:T(4,128)} %param.8) | copy-start | bytes 18436
  101.0 1.6 copy-start.4
  101.0 2.2 %copy-start.2 = (s32[512]{0:T(512)S(1)}, s32[512]{0:T(512)}, u32[]{:S(2)}) copy-start(s32[512]{0:T(512)} %param.11) | copy-start | bytes 6148
  113.2 78.9 %copy-start.3 = (s32[128]{0:T(128)S(1)}, s32[128]{0:T(128)}, u32[]{:S(2)}) copy-start(s32[128]{0:T(128)} %param.13) | copy-start | bytes 1540
Sparse Core Ops, SparseCore 0:
  11.0 94.6 all-gather.2
